TPU v7x, 32 devices: a whole 2x2x4 slice. The times are simulated.
32 devices in a mesh: net: 4 (over y, x), line: 8 (over z, core).
Axes of the slice: x: 2, y: 2, z: 4, core: 2. Of those that a mesh axis runs over, the one named last changes fastest.
Arguments:
- conductance_inverse: float32 [4, 4096, 4096], P('net', 'line'), may hold values from -0.5 to 4.5, as said below
- prior_voltage: float32 [4, 96, 4096], P('net', None, 'line'), may hold values from -6 to 6
- sources: float32 [3, 4, 4096], P(None, 'net', 'line'), may hold values from -6 to 6
- fault_node: int32 [96], replicated, may hold values from 0 to 16383
- fault_conductance: float32 [96], replicated, may hold values from 0.5 to 4
- terminal_node: int32 [4, 3, 4096], P('net', None, 'line'), may hold values from 0 to 4095
- ownership: int32 [4, 4096], P('net', 'line'), may hold values from 0 to 1, as said below
- partner: int32 [4, 4096], P('net', 'line'), may hold values from 0 to 31, as said below
- delay_steps: int32 [4, 4096], P('net', 'line'), may hold values from 1 to 4, as said below
- surge_conductance: float32 [4, 4096], P('net', 'line'), may hold values from 0.2 to 1
- pole_wave: float32 [4, 6, 4096], P('net', None, 'line'), may hold values from 0.2 to 0.95
- residue_wave: float32 [4, 6, 3, 3, 4096], P('net', None, None, None, 'line'), may hold values from -1 to 1
- pole_admit: float32 [4, 6, 4096], P('net', None, 'line'), may hold values from 0.2 to 0.95
- residue_admit: float32 [4, 6, 3, 3, 4096], P('net', None, None, None, 'line'), may hold values from -1 to 1
- wave_state: float32 [4, 6, 3, 96, 4096], P('net', None, None, None, 'line'), may hold values from -4 to 4
- admit_state: float32 [4, 6, 3, 96, 4096], P('net', None, None, None, 'line'), may hold values from -4 to 4
- wave_history: float32 [4, 4, 3, 96, 4096], P('net', None, None, None, 'line'), may hold values from -6 to 6
Outputs:
- final_voltage: float32 [4, 96, 4096], P('net', None, 'line')
- end_current: float32 [4, 3, 96, 4096], P('net', None, None, 'line')
Inputs may be any that keep to these rules, and one draw needn't show every extreme that they name: `conductance_inverse`: each block is exactly symmetric. `ownership`: A slot is live exactly when the slot of the same number j % 512 at its partner owner is live; the number of live slots differs from owner to owner. The far end of slot j lies in the slot of the same number j % 512 at the partner owner, the partner of that slot is the first owner again, never the owner itself, and at most 17 live slots of one owner have the same partner; this many occur. `delay_steps`: equal at both ends of a line.
All inputs are finite; a program needn't handle non-finite values.
Results may differ from a plain program's by a relative error of at most 0.0003.
Values sent between devices are 32-bit elements; how exact they have to be, the bound alone decides.
A program may use at most 128 MiB of HBM per device.

v0:
```python
import jax
import jax.numpy as jnp
from jax import lax
from jax.sharding import PartitionSpec as P

STEPS = 3


def mix_residue(residue, vector):
    return (
        residue[:, :, 0, None, :] * vector[0]
        + residue[:, :, 1, None, :] * vector[1]
        + residue[:, :, 2, None, :] * vector[2]
    )


def select_delayed(buffer, delay_local):
    depth_count = buffer.shape[0]
    chosen = delay_local[None, :] == jnp.arange(1, depth_count + 1, dtype=jnp.int32)[:, None]
    return jnp.sum(jnp.where(chosen[:, None, None, :], buffer, 0.0), axis=0)


def terminal_values(voltage, terminal):
    picked = jnp.take(voltage, terminal.reshape(-1), axis=1)
    return jnp.moveaxis(picked.reshape(voltage.shape[0], 3, -1), 0, 1)


def spread_ends(history, terminal, node_count):
    values = jnp.moveaxis(history, 0, 1).reshape(history.shape[1], -1)
    return (
        jnp.zeros((history.shape[1], node_count), jnp.float32)
        .at[:, terminal.reshape(-1)]
        .add(values)
    )


def gather_full(block):
    return lax.all_gather(block, "line", axis=1, tiled=True)


def on_device(
    conductance_inverse,
    prior_voltage,
    sources,
    fault_node,
    fault_conductance,
    terminal_node,
    ownership,
    partner,
    delay_steps,
    surge_conductance,
    pole_wave,
    residue_wave,
    pole_admit,
    residue_admit,
    wave_state,
    admit_state,
    wave_history,
):
    inverse_block = conductance_inverse[0]
    row_count = inverse_block.shape[0]
    node_count = inverse_block.shape[1]
    line_index = lax.axis_index("line")
    net_index = lax.axis_index("net")
    offset = line_index * row_count
    net_count = lax.axis_size("net")
    line_count = lax.axis_size("line")
    devices = net_count * line_count
    slot_count = ownership.shape[1]
    capacity = (slot_count + devices - 2) // (devices - 1)
    is_live = ownership[0] > 0
    live_float = is_live.astype(jnp.float32)
    terminal = terminal_node[0]
    delay_local = delay_steps[0]
    surge_local = surge_conductance[0]
    partners = partner[0]
    slot_range = jnp.arange(slot_count, dtype=jnp.int32)
    earlier = (
        (partners[:, None] == partners[None, :])
        & is_live[None, :]
        & (slot_range[None, :] < slot_range[:, None])
    )
    slot_rank = jnp.sum(earlier.astype(jnp.int32), axis=1)
    position = jnp.where(is_live, partners * capacity + slot_rank, devices * capacity)
    scenario_range = jnp.arange(prior_voltage.shape[1], dtype=jnp.int32)
    fault_sub = fault_node // node_count
    fault_local = fault_node % node_count
    fault_here = (fault_sub == net_index) & (fault_local // row_count == line_index)
    wave_decay = pole_wave[0][:, None, None, :]
    admit_decay = pole_admit[0][:, None, None, :]
    wave_res = residue_wave[0]
    admit_res = residue_admit[0]
    voltage = gather_full(prior_voltage[0])
    voltage_rows = prior_voltage[0]
    wave_now = wave_state[0]
    admits = admit_state[0]
    history_buffer = wave_history[0]
    outgoing = None
    current = None
    for step_index in range(STEPS):
        terminal_prior = terminal_values(voltage, terminal)
        admits = admit_decay * admits + mix_residue(admit_res, terminal_prior)
        if step_index == 0:
            wave_now = wave_decay * wave_now + mix_residue(
                wave_res, select_delayed(history_buffer, delay_local)
            )
        else:
            shifted = jnp.concatenate(
                [jnp.zeros_like(history_buffer[:1]), history_buffer[:-1]], axis=0
            )
            wave_now = wave_decay * wave_now + mix_residue(
                wave_res, select_delayed(shifted, delay_local)
            )
            row_width = outgoing.shape[0] * outgoing.shape[1]
            packed = jnp.moveaxis(outgoing, 2, 0).reshape(slot_count, row_width)
            buffer = (
                jnp.zeros((devices * capacity, row_width), jnp.float32)
                .at[position]
                .set(packed, mode="drop")
            )
            arrived = lax.all_to_all(
                buffer, ("net", "line"), split_axis=0, concat_axis=0, tiled=True
            )
            picked_rows = arrived[jnp.minimum(position, devices * capacity - 1)]
            arrived = jnp.moveaxis(picked_rows.reshape(slot_count, 3, -1), 0, 2) * live_float
            newest = jnp.where((delay_local == 1)[None, None, :], arrived, 0.0)
            wave_now = wave_now + mix_residue(wave_res, newest)
            history_buffer = jnp.concatenate([arrived[None], shifted[1:]], axis=0)
        history = (jnp.sum(wave_now, axis=0) - jnp.sum(admits, axis=0)) * live_float
        injection = spread_ends(history, terminal, node_count)
        own_part = (
            lax.dynamic_slice_in_dim(injection, offset, row_count, 1)
            + sources[step_index, 0][None, :]
        )
        injection = lax.dynamic_update_slice_in_dim(injection, own_part, offset, 1)
        fault_value = voltage[scenario_range, fault_local]
        injection = injection.at[scenario_range, fault_local].add(
            jnp.where(fault_here, -fault_conductance * fault_value, 0.0)
        )
        summed = lax.psum(injection, "line")
        voltage_rows = lax.dot_general(
            summed,
            inverse_block,
            (((1,), (1,)), ((), ())),
            precision=lax.Precision.HIGHEST,
            preferred_element_type=jnp.float32,
        )
        voltage = gather_full(voltage_rows)
        terminal_now = terminal_values(voltage, terminal)
        if step_index + 1 < STEPS:
            outgoing = (2.0 * surge_local * terminal_now - history) * live_float
        else:
            current = (surge_local * terminal_now - history) * live_float
    return (voltage_rows[None], current[None])


def solution(mesh):
    return jax.shard_map(
        on_device,
        mesh=mesh,
        in_specs=(
            P("net", "line", None),
            P("net", None, "line"),
            P(None, "net", "line"),
            P(),
            P(),
            P("net", None, "line"),
            P("net", "line"),
            P("net", "line"),
            P("net", "line"),
            P("net", "line"),
            P("net", None, "line"),
            P("net", None, None, None, "line"),
            P("net", None, "line"),
            P("net", None, None, None, "line"),
            P("net", None, None, None, "line"),
            P("net", None, None, None, "line"),
            P("net", None, None, None, "line"),
        ),
        out_specs=(P("net", None, "line"), P("net", None, None, "line")),
        check_vma=False,
    )
```

profile of v0, /device:TPU:0, one launch (start us, length us, event | category | flops | bytes accessed | tf_op | source)
XLA Modules:
  0.0 577.8 jit_solution(13432879487147559588)
XLA Ops:
  32.9 8.7 %all-gather.12.cloned.1.call-done = f32[1,96,4096]{1,2,0:T(8,128)} async-done(((f32[1,96,512]{1,2,0:T(8,128)}), f32[1,96,4096]{1,2,0:T(8,128)}) %all-gather.12.cloned.1.call-update) | async-done | bytes 1572880 | tf_op jit(solution)/shard_map/all_gather | solution.py:38
  45.1 5.6 gather_fusion.5
  64.7 10.5 %scatter_custom_fusion = f32[96,4096]{0,1:T(8,128)} fusion(s32[1536]{0:T(1024)} %fusion.32, f32[1536,96]{1,0:T(8,128)} %copy.74, f32[]{:T(128)} %constant.37.clone.1), kind=kCustom, calls=%fused_computation.47 | custom fusion | flops 147456 | bytes 1573376 | tf_op jit(solution)/shard_map/scatter-add | solution.py:33
  81.1 12.2 %scatter_fusion = f32[96,4096]{1,0:T(8,128)} fusion(f32[96,4096]{1,0:T(8,128)} %copy.75, s32[96]{0:T(128)S(1)} %fusion.36, f32[96]{0:T(128)} %get-tuple-element.9), kind=kCustom, calls=%fused_computation.10 | custom fusion | flops 96 | bytes 1920 | tf_op jit(solution)/shard_map/scatter-add | solution.py:137
  93.6 61.2 %all-reduce.6.cloned.1.call-done = f32[96,4096]{1,0:T(8,128)} async-done(((f32[96,4096]{1,0:T(8,128)}), f32[96,4096]{1,0:T(8,128)}) %all-reduce.6.cloned.1.call-update) | async-done | bytes 1572880 | tf_op jit(solution)/shard_map/psum | solution.py:140
  154.8 12.7 %fusion.4 = f32[96,512]{1,0:T(8,128)} fusion(f32[96,4096]{1,0:T(8,128)} %all-reduce.6.cloned.1.call-done, f32[1,512,4096]{2,1,0:T(8,128)} %param.19), kind=kOutput, calls=%fused_computation.21 | convolution fusion | flops 2415919104 | bytes 10158080 | tf_op jit(solution)/shard_map/dot_general | solution.py:141
  174.4 17.7 %all-gather.6.cloned.1.call-done = f32[96,4096]{1,0:T(8,128)} async-done(((f32[96,512]{1,0:T(8,128)}), f32[96,4096]{1,0:T(8,128)}) %all-gather.6.cloned.1.call-update) | async-done | bytes 1572880 | tf_op jit(solution)/shard_map/all_gather | solution.py:38
  194.9 5.6 gather_fusion.6
  215.7 3.8 all-to-all-start
  234.3 4.2 fusion.11
  238.5 11.3 %all-to-all-done = f32[32,17,288]{2,1,0:T(8,128)} async-done(((f32[32,17,288]{2,1,0:T(8,128)}), f32[32,17,288]{2,1,0:T(8,128)}, u32[]{:S(2)}, u32[]{:S(2)}) %all-to-all-start) | async-done | bytes 626720 | tf_op jit(solution)/shard_map/all_to_all | solution.py:121
  256.8 3.9 fusion.38
  262.1 9.4 %scatter_custom_fusion.3 = f32[96,4096]{0,1:T(8,128)S(1)} fusion(s32[1536]{0:T(1024)} %fusion.32, f32[1536,96]{1,0:T(8,128)S(1)} %copy.84, f32[]{:T(128)} %constant.37.clone.1), kind=kCustom, calls=%fused_computation.45 | custom fusion | flops 147456 | bytes 1573376 | tf_op jit(solution)/shard_map/scatter-add | solution.py:33
  273.3 12.2 %scatter_fusion.1 = f32[96,4096]{1,0:T(8,128)} fusion(f32[96,4096]{1,0:T(8,128)} %copy.85, s32[96]{0:T(128)S(1)} %fusion.36, f32[96]{0:T(128)S(1)} %copy-done.45), kind=kCustom, calls=%fused_computation.13 | custom fusion | flops 96 | bytes 1920 | tf_op jit(solution)/shard_map/scatter-add | solution.py:137
  286.0 59.3 %all-reduce.8.cloned.1.call-done = f32[96,4096]{1,0:T(8,128)} async-done(((f32[96,4096]{1,0:T(8,128)}), f32[96,4096]{1,0:T(8,128)}) %all-reduce.8.cloned.1.call-update) | async-done | bytes 1572880 | tf_op jit(solution)/shard_map/psum | solution.py:140
  345.3 12.6 %fusion.2 = f32[96,512]{1,0:T(8,128)} fusion(f32[96,4096]{1,0:T(8,128)} %all-reduce.8.cloned.1.call-done, f32[1,512,4096]{2,1,0:T(8,128)} %param.19), kind=kOutput, calls=%fused_computation.19 | convolution fusion | flops 2415919104 | bytes 10158080 | tf_op jit(solution)/shard_map/dot_general | solution.py:141
  358.8 23.8 %all-gather.8.cloned.1.call-done = f32[96,4096]{1,0:T(8,128)} async-done(((f32[96,512]{1,0:T(8,128)}), f32[96,4096]{1,0:T(8,128)}) %all-gather.8.cloned.1.call-update) | async-done | bytes 1572880 | tf_op jit(solution)/shard_map/all_gather | solution.py:38
  412.3 4.8 add_reduce_fusion
  417.2 13.2 %all-to-all-done.1 = f32[32,17,288]{2,1,0:T(8,128)} async-done(((f32[32,17,288]{2,1,0:T(8,128)}), f32[32,17,288]{2,1,0:T(8,128)}, u32[]{:S(2)}, u32[]{:S(2)}) %all-to-all-start.1) | async-done | bytes 626720 | tf_op jit(solution)/shard_map/all_to_all | solution.py:121
  442.0 9.4 %scatter_custom_fusion.6 = f32[96,4096]{0,1:T(8,128)S(1)} fusion(s32[1536]{0:T(1024)} %fusion.32, f32[1536,96]{1,0:T(8,128)S(1)} %copy.94, f32[]{:T(128)} %constant.37.clone.1), kind=kCustom, calls=%fused_computation.43 | custom fusion | flops 147456 | bytes 1573376 | tf_op jit(solution)/shard_map/scatter-add | solution.py:33
  453.2 12.2 %scatter_fusion.2 = f32[96,4096]{1,0:T(8,128)} fusion(f32[96,4096]{1,0:T(8,128)} %copy.95, s32[96]{0:T(128)S(1)} %fusion.36, f32[96]{0:T(128)S(1)} %copy-done.44), kind=kCustom, calls=%fused_computation.16 | custom fusion | flops 96 | bytes 1920 | tf_op jit(solution)/shard_map/scatter-add | solution.py:137
  465.7 59.5 %all-reduce.10.cloned.1.call-done = f32[96,4096]{1,0:T(8,128)} async-done(((f32[96,4096]{1,0:T(8,128)}), f32[96,4096]{1,0:T(8,128)}) %all-reduce.10.cloned.1.call-update) | async-done | bytes 1572880 | tf_op jit(solution)/shard_map/psum | solution.py:140
  525.2 12.7 %fusion = f32[96,512]{1,0:T(8,128)} fusion(f32[96,4096]{1,0:T(8,128)} %all-reduce.10.cloned.1.call-done, f32[1,512,4096]{2,1,0:T(8,128)} %param.19), kind=kOutput, calls=%fused_computation.17 | convolution fusion | flops 2415919104 | bytes 10158080 | tf_op jit(solution)/shard_map/dot_general | solution.py:141
  537.9 24.6 %all-gather.10.cloned.1.call-done = f32[96,4096]{1,0:T(8,128)} async-done(((f32[96,512]{1,0:T(8,128)}), f32[96,4096]{1,0:T(8,128)}) %all-gather.10.cloned.1.call-update) | async-done | bytes 1572880 | tf_op jit(solution)/shard_map/all_gather | solution.py:38
  (215 shorter events, 151.6 us)
Async XLA Ops:
  7.2 18.5 %copy-start.46 = (s32[96]{0:T(128)S(1)}, s32[96]{0:T(128)}, u32[]{:S(2)}) copy-start(s32[96]{0:T(128)} %param.22) | copy-start | bytes 1156
  7.2 23.8 %copy-start.2 = (f32[1,6,3,96,512]{4,3,2,1,0:T(8,128)S(1)}, f32[1,6,3,96,512]{4,3,2,1,0:T(8,128)}, u32[]{:S(2)}) copy-start(f32[1,6,3,96,512]{4,3,2,1,0:T(8,128)} %param.33) | copy-start | bytes 10616836
  7.2 34.3 %all-gather.12.cloned.1.call-start = ((), (), s32[]{:S(2)}) async-start(), calls=%async_computation.8 | async-start | bytes 2359296 | tf_op jit(solution)/shard_map/all_gather | solution.py:38
  9.2 145.6 %all-reduce.6.cloned.1.call-start = ((), (), s32[]{:S(2)}) async-start(), calls=%async_computation.2 | async-start | bytes 3145728 | tf_op jit(solution)/shard_map/psum | solution.py:140
  12.5 11.2 %copy-start.35 = (s32[1536]{0:T(1024)}, s32[1536]{0:T(1024)S(1)}, u32[]{:S(2)}) copy-start(s32[1536]{0:T(1024)S(1)} %reshape_squeeze.5) | copy-start | bytes 18436
  20.2 10.8 %copy-start.25 = (f32[6,3,1,512]{3,1,2,0:T(4,128)S(1)}, f32[6,3,1,512]{3,1,2,0:T(4,128)}, u32[]{:S(2)}) copy-start(f32[6,3,1,512]{3,1,2,0:T(4,128)} %copy.124) | copy-start | bytes 110596
  20.2 10.8 %copy-start.31 = (f32[1,6,512]{2,1,0:T(8,128)S(1)}, f32[1,6,512]{2,1,0:T(8,128)}, u32[]{:S(2)}) copy-start(f32[1,6,512]{2,1,0:T(8,128)} %copy.126) | copy-start | bytes 36868
  50.7 7.7 %copy-start = (f32[1,6,3,96,512]{4,3,2,1,0:T(8,128)S(1)}, f32[1,6,3,96,512]{4,3,2,1,0:T(8,128)}, u32[]{:S(2)}) copy-start(f32[1,6,3,96,512]{4,3,2,1,0:T(8,128)} %param.34) | copy-start | bytes 10616836
  93.4 98.7 %all-gather.6.cloned.1.call-start = ((), (), s32[]{:S(2)}) async-start(), calls=%async_computation.3 | async-start | bytes 1769472 | tf_op jit(solution)/shard_map/all_gather | solution.py:38
  215.7 34.1 %all-to-all-start = ((f32[32,17,288]{2,1,0:T(8,128)}), f32[32,17,288]{2,1,0:T(8,128)}, u32[]{:S(2)}, u32[]{:S(2)}) async-start(f32[32,17,288]{2,1,0:T(8,128)} %all_to_all.16), calls=%async_computation | async-start | bytes 2359296 | tf_op jit(solution)/shard_map/all_to_all | solution.py:121
  219.5 125.8 %all-reduce.8.cloned.1.call-start = ((), (), s32[]{:S(2)}) async-start(), calls=%async_computation.4 | async-start | bytes 3145728 | tf_op jit(solution)/shard_map/psum | solution.py:140
  260.8 10.7 %copy-start.41 = (f32[1,1,512]{2,1,0:T(1,128)S(1)}, f32[1,1,512]{2,1,0:T(1,128)}, u32[]{:S(2)}) copy-start(f32[1,1,512]{2,1,0:T(1,128)} %get-tuple-element.45) | copy-start | bytes 6148
  261.8 11.6 %copy-start.45 = (f32[96]{0:T(128)S(1)}, f32[96]{0:T(128)}, u32[]{:S(2)}) copy-start(f32[96]{0:T(128)} %multiply_select_fusion.1) | copy-start | bytes 1156
  285.6 72.4 %copy-start.18 = (f32[3,96,512]{2,1,0:T(8,128)S(1)}, f32[3,96,512]{2,1,0:T(8,128)}, u32[]{:S(2)}) copy-start(f32[3,96,512]{2,1,0:T(8,128)} %get-tuple-element.3) | copy-start | bytes 1769476
  285.6 97.0 %all-gather.8.cloned.1.call-start = ((), (), s32[]{:S(2)}) async-start(), calls=%async_computation.5 | async-start | bytes 1769472 | tf_op jit(solution)/shard_map/all_gather | solution.py:38
  358.0 26.5 %copy-start.33 = (s32[2048]{0:T(1024)S(1)}, s32[2048]{0:T(1024)}, u32[]{:S(2)}) copy-start(s32[2048]{0:T(1024)} %pad_clamp_fusion) | copy-start | bytes 24580
  384.4 5.4 copy-start.11
  393.8 18.5 %copy-start.1 = (f32[1,6,3,96,512]{4,3,2,1,0:T(8,128)S(1)}, f32[1,6,3,96,512]{4,3,2,1,0:T(8,128)}, u32[]{:S(2)}) copy-start(f32[1,6,3,96,512]{4,3,2,1,0:T(8,128)} %param.34) | copy-start | bytes 10616836
  396.3 34.1 %all-to-all-start.1 = ((f32[32,17,288]{2,1,0:T(8,128)}), f32[32,17,288]{2,1,0:T(8,128)}, u32[]{:S(2)}, u32[]{:S(2)}) async-start(f32[32,17,288]{2,1,0:T(8,128)} %all_to_all.19), calls=%async_computation.1 | async-start | bytes 2359296 | tf_op jit(solution)/shard_map/all_to_all | solution.py:121
  400.1 125.1 %all-reduce.10.cloned.1.call-start = ((), (), s32[]{:S(2)}) async-start(), calls=%async_computation.6 | async-start | bytes 3145728 | tf_op jit(solution)/shard_map/psum | solution.py:140
  440.8 10.5 %copy-start.40 = (f32[1,1,512]{2,1,0:T(1,128)S(1)}, f32[1,1,512]{2,1,0:T(1,128)}, u32[]{:S(2)}) copy-start(f32[1,1,512]{2,1,0:T(1,128)} %get-tuple-element.43) | copy-start | bytes 6148
  441.7 11.5 %copy-start.44 = (f32[96]{0:T(128)S(1)}, f32[96]{0:T(128)}, u32[]{:S(2)}) copy-start(f32[96]{0:T(128)} %multiply_select_fusion) | copy-start | bytes 1156
  465.5 97.0 %all-gather.10.cloned.1.call-start = ((), (), s32[]{:S(2)}) async-start(), calls=%async_computation.7 | async-start | bytes 1769472 | tf_op jit(solution)/shard_map/all_gather | solution.py:38
  537.9 26.5 %copy-start.34 = (s32[2048]{0:T(1024)S(1)}, s32[2048]{0:T(1024)}, u32[]{:S(2)}) copy-start(s32[2048]{0:T(1024)} %pad_clamp_fusion) | copy-start | bytes 24580
  (33 other events, 88.0 us)
Sparse Core Ops, SparseCore 0:
  9.6 31.8 all-gather.11
  93.5 61.2 all-reduce.5
  167.6 24.4 all-gather.5
  285.7 59.5 all-reduce.7
  358.1 24.4 all-gather.7
  465.6 59.5 all-reduce.9
  538.0 24.4 all-gather.9
where the time goes:
time: 587 us; the launch traced here: 578 us
  waiting for transfers between devices  279 us (48%)
  other arithmetic  122 us (21%)
  local copies, waits for them, and re-layouts  115 us (20%)
  matrix products  38 us (6%)
  between operations  15.2 us (3%)
  starting transfers between devices  9.15 us (2%)
    psum x3, waiting for transfers between devices, on_device(): summed = lax.psum(injection, 'line')  180 us
    all_gather x4, waiting for transfers between devices, gather_full(): return lax.all_gather(block, 'line', axis=1, tiled=True)  74.8 us
    dot_general x3, matrix products, on_device(): lax.dot_general(summed, inverse_block, (((1,), (1,)), ((), ())), precisio...  38 us
    scatter-add x3, other arithmetic, on_device(): injection.at[scenario_range, fault_local]  36.6 us
    scatter-add x3, other arithmetic, spread_ends(): return jnp.zeros((history.shape[1], node_count), jnp.float32).at[:, termi...  29.3 us
    all_to_all x2, waiting for transfers between devices, on_device(): lax.all_to_all(buffer, ('net', 'line'), split_axis=0, concat_axis=0, tile...  24.6 us
    reduce_sum x6, other arithmetic, on_device(): history = (jnp.sum(wave_now, axis=0) - jnp.sum(admits, axis=0)) * live_float  20.3 us
    gather x4, local copies, waits for them, and re-layouts, terminal_values(): picked = jnp.take(voltage, terminal.reshape(-1), axis=1)  18.5 us
  transfers between devices with their start and end apart: 9, of which 9 were waited for; matrix products, arithmetic and copies ran while one was open for 11% of the time, Pallas kernels for 0%

commit v1 on v0

--- a/solution.py
+++ b/solution.py
@@ -137,7 +137,15 @@
         injection = injection.at[scenario_range, fault_local].add(
             jnp.where(fault_here, -fault_conductance * fault_value, 0.0)
         )
-        summed = lax.psum(injection, "line")
+        num = lax.axis_size("line")
+        summed, arr_out = (injection, 0)
+        while 1 << arr_out < num:
+            parts_seen = []
+            for ii in range(num):
+                parts_seen.append((ii, ii ^ 1 << arr_out))
+            tile_out = lax.ppermute(summed, "line", parts_seen)
+            summed = summed + tile_out
+            arr_out = arr_out + 1
         voltage_rows = lax.dot_general(
             summed,
             inverse_block,

time: 587 us -> 735 us (1.25)
  waiting for transfers between devices: 279 us -> 424 us
    ppermute x0 -> x9, waiting for transfers between devices: none -> 327 us  [on_device(): tile_out = lax.ppermute(summed, 'line', parts_seen)]
    psum x3 -> x0, waiting for transfers between devices: 180 us -> none  [on_device(): summed = lax.psum(injection, 'line')]
  transfers between devices with their start and end apart: 9 -> 15, of which waited for: 9 -> 15; matrix products, arithmetic and copies ran while one was open for 11% -> 9% of each run, Pallas kernels for 0% -> 0%
where the time goes in v1:
time: 735 us; the launch traced here: 726 us
  waiting for transfers between devices  424 us (58%)
  other arithmetic  127 us (17%)
  local copies, waits for them, and re-layouts  115 us (16%)
  matrix products  33.6 us (5%)
  between operations  15.1 us (2%)
  starting transfers between devices  12.2 us (2%)
    ppermute x9, waiting for transfers between devices, on_device(): tile_out = lax.ppermute(summed, 'line', parts_seen)  327 us
    all_gather x4, waiting for transfers between devices, gather_full(): return lax.all_gather(block, 'line', axis=1, tiled=True)  71.8 us
    scatter-add x3, other arithmetic, on_device(): injection.at[scenario_range, fault_local]  36.7 us
    dot_general x3, matrix products, on_device(): lax.dot_general(summed, inverse_block, (((1,), (1,)), ((), ())), precisio...  33.6 us
    scatter-add x3, other arithmetic, spread_ends(): return jnp.zeros((history.shape[1], node_count), jnp.float32).at[:, termi...  30.5 us
    all_to_all x2, waiting for transfers between devices, on_device(): lax.all_to_all(buffer, ('net', 'line'), split_axis=0, concat_axis=0, tile...  24.5 us
    reduce_sum x6, other arithmetic, on_device(): history = (jnp.sum(wave_now, axis=0) - jnp.sum(admits, axis=0)) * live_float  20.3 us
    gather x4, local copies, waits for them, and re-layouts, terminal_values(): picked = jnp.take(voltage, terminal.reshape(-1), axis=1)  18.5 us
  transfers between devices with their start and end apart: 15, of which 15 were waited for; matrix products, arithmetic and copies ran while one was open for 9% of the time, Pallas kernels for 0%

profile of v1, /device:TPU:0, one launch (start us, length us, event | category | flops | bytes accessed | tf_op | source)
XLA Modules:
  0.0 726.3 jit_solution(3643741070859684946)
XLA Ops:
  32.9 8.6 %all-gather.12.cloned.1.call-done = f32[1,96,4096]{1,2,0:T(8,128)} async-done(((f32[1,96,512]{1,2,0:T(8,128)}), f32[1,96,4096]{1,2,0:T(8,128)}) %all-gather.12.cloned.1.call-update) | async-done | bytes 1572880 | tf_op jit(solution)/shard_map/all_gather | solution.py:38
  45.1 5.6 gather_fusion.5
  64.8 11.0 %scatter_custom_fusion = f32[96,4096]{0,1:T(8,128)} fusion(s32[1536]{0:T(1024)} %fusion.35, f32[1536,96]{1,0:T(8,128)} %copy.74, f32[]{:T(128)} %constant.37.clone.1), kind=kCustom, calls=%fused_computation.50 | custom fusion | flops 147456 | bytes 1573376 | tf_op jit(solution)/shard_map/scatter-add | solution.py:33
  81.6 12.2 %scatter_fusion = f32[96,4096]{1,0:T(8,128)} fusion(f32[96,4096]{1,0:T(8,128)} %copy.75, s32[96]{0:T(128)S(1)} %fusion.39, f32[96]{0:T(128)} %get-tuple-element.9), kind=kCustom, calls=%fused_computation.10 | custom fusion | flops 96 | bytes 1920 | tf_op jit(solution)/shard_map/scatter-add | solution.py:137
  100.6 35.1 %collective-permute-done.1 = f32[96,4096]{1,0:T(8,128)S(1)} collective-permute-done((f32[96,4096]{1,0:T(8,128)S(1)}, f32[96,4096]{1,0:T(8,128)S(1)}, u32[]{:S(2)}, u32[]{:S(2)}) %collective-permute-start.1) | collective-permute-done | bytes 1572896 | tf_op jit(solution)/shard_map/ppermute | solution.py:146
  137.7 68.5 %collective-permute-done.2 = f32[96,4096]{1,0:T(8,128)S(1)} collective-permute-done((f32[96,4096]{1,0:T(8,128)S(1)}, f32[96,4096]{1,0:T(8,128)S(1)}, u32[]{:S(2)}, u32[]{:S(2)}) %collective-permute-start.2) | collective-permute-done | bytes 1572896 | tf_op jit(solution)/shard_map/ppermute | solution.py:146
  206.2 11.2 %fusion.4 = f32[96,512]{1,0:T(8,128)} fusion(f32[1,512,4096]{2,1,0:T(8,128)} %param.19, f32[96,4096]{1,0:T(8,128)S(1)} %add.258, f32[96,4096]{1,0:T(8,128)S(1)} %collective-permute-done.2), kind=kOutput, calls=%fused_computation.21 | convolution fusion | flops 2416312320 | bytes 11730944 | tf_op jit(solution)/shard_map/dot_general | solution.py:149
  224.4 17.8 %all-gather.6.cloned.1.call-done = f32[96,4096]{1,0:T(8,128)} async-done(((f32[96,512]{1,0:T(8,128)}), f32[96,4096]{1,0:T(8,128)}) %all-gather.6.cloned.1.call-update) | async-done | bytes 1572880 | tf_op jit(solution)/shard_map/all_gather | solution.py:38
  245.0 5.6 gather_fusion.6
  288.5 11.4 %all-to-all-done = f32[32,17,288]{2,1,0:T(8,128)} async-done(((f32[32,17,288]{2,1,0:T(8,128)}), f32[32,17,288]{2,1,0:T(8,128)}, u32[]{:S(2)}, u32[]{:S(2)}) %all-to-all-start) | async-done | bytes 626720 | tf_op jit(solution)/shard_map/all_to_all | solution.py:121
  311.1 9.8 %scatter_custom_fusion.3 = f32[96,4096]{0,1:T(8,128)S(1)} fusion(s32[1536]{0:T(1024)} %fusion.35, f32[1536,96]{1,0:T(8,128)} %copy.84, f32[]{:T(128)} %constant.37.clone.1), kind=kCustom, calls=%fused_computation.48 | custom fusion | flops 147456 | bytes 1573376 | tf_op jit(solution)/shard_map/scatter-add | solution.py:33
  322.8 12.2 %scatter_fusion.1 = f32[96,4096]{1,0:T(8,128)} fusion(f32[96,4096]{1,0:T(8,128)} %copy.85, s32[96]{0:T(128)S(1)} %fusion.39, f32[96]{0:T(128)S(1)} %copy-done.42), kind=kCustom, calls=%fused_computation.13 | custom fusion | flops 96 | bytes 1920 | tf_op jit(solution)/shard_map/scatter-add | solution.py:137
  340.3 36.4 %collective-permute-done.4 = f32[96,4096]{1,0:T(8,128)S(1)} collective-permute-done((f32[96,4096]{1,0:T(8,128)S(1)}, f32[96,4096]{1,0:T(8,128)S(1)}, u32[]{:S(2)}, u32[]{:S(2)}) %collective-permute-start.4) | collective-permute-done | bytes 1572896 | tf_op jit(solution)/shard_map/ppermute | solution.py:146
  377.0 70.2 %collective-permute-done.5 = f32[96,4096]{1,0:T(8,128)S(1)} collective-permute-done((f32[96,4096]{1,0:T(8,128)S(1)}, f32[96,4096]{1,0:T(8,128)S(1)}, u32[]{:S(2)}, u32[]{:S(2)}) %collective-permute-start.5) | collective-permute-done | bytes 1572896 | tf_op jit(solution)/shard_map/ppermute | solution.py:146
  447.2 11.2 %fusion.2 = f32[96,512]{1,0:T(8,128)} fusion(f32[1,512,4096]{2,1,0:T(8,128)} %param.19, f32[96,4096]{1,0:T(8,128)S(1)} %add.274, f32[96,4096]{1,0:T(8,128)S(1)} %collective-permute-done.5), kind=kOutput, calls=%fused_computation.19 | convolution fusion | flops 2416312320 | bytes 11730944 | tf_op jit(solution)/shard_map/dot_general | solution.py:149
  459.3 22.2 %all-gather.8.cloned.1.call-done = f32[96,4096]{1,0:T(8,128)} async-done(((f32[96,512]{1,0:T(8,128)}), f32[96,4096]{1,0:T(8,128)}) %all-gather.8.cloned.1.call-update) | async-done | bytes 1572880 | tf_op jit(solution)/shard_map/all_gather | solution.py:38
  511.3 4.8 add_reduce_fusion
  516.1 13.1 %all-to-all-done.1 = f32[32,17,288]{2,1,0:T(8,128)} async-done(((f32[32,17,288]{2,1,0:T(8,128)}), f32[32,17,288]{2,1,0:T(8,128)}, u32[]{:S(2)}, u32[]{:S(2)}) %all-to-all-start.1) | async-done | bytes 626720 | tf_op jit(solution)/shard_map/all_to_all | solution.py:121
  540.8 9.7 %scatter_custom_fusion.6 = f32[96,4096]{0,1:T(8,128)S(1)} fusion(s32[1536]{0:T(1024)} %fusion.35, f32[1536,96]{1,0:T(8,128)S(1)} %copy.94, f32[]{:T(128)} %constant.37.clone.1), kind=kCustom, calls=%fused_computation.46 | custom fusion | flops 147456 | bytes 1573376 | tf_op jit(solution)/shard_map/scatter-add | solution.py:33
  552.3 12.2 %scatter_fusion.2 = f32[96,4096]{1,0:T(8,128)} fusion(f32[96,4096]{1,0:T(8,128)} %copy.95, s32[96]{0:T(128)S(1)} %fusion.39, f32[96]{0:T(128)S(1)} %copy-done.41), kind=kCustom, calls=%fused_computation.16 | custom fusion | flops 96 | bytes 1920 | tf_op jit(solution)/shard_map/scatter-add | solution.py:137
  569.8 36.4 %collective-permute-done.7 = f32[96,4096]{1,0:T(8,128)S(1)} collective-permute-done((f32[96,4096]{1,0:T(8,128)S(1)}, f32[96,4096]{1,0:T(8,128)S(1)}, u32[]{:S(2)}, u32[]{:S(2)}) %collective-permute-start.7) | collective-permute-done | bytes 1572896 | tf_op jit(solution)/shard_map/ppermute | solution.py:146
  606.5 70.2 %collective-permute-done.8 = f32[96,4096]{1,0:T(8,128)S(1)} collective-permute-done((f32[96,4096]{1,0:T(8,128)S(1)}, f32[96,4096]{1,0:T(8,128)S(1)}, u32[]{:S(2)}, u32[]{:S(2)}) %collective-permute-start.8) | collective-permute-done | bytes 1572896 | tf_op jit(solution)/shard_map/ppermute | solution.py:146
  676.7 11.2 %fusion = f32[96,512]{1,0:T(8,128)} fusion(f32[1,512,4096]{2,1,0:T(8,128)} %param.19, f32[96,4096]{1,0:T(8,128)S(1)} %add.286, f32[96,4096]{1,0:T(8,128)S(1)} %collective-permute-done.8), kind=kOutput, calls=%fused_computation.17 | convolution fusion | flops 2416312320 | bytes 11730944 | tf_op jit(solution)/shard_map/dot_general | solution.py:149
  687.9 23.1 %all-gather.10.cloned.1.call-done = f32[96,4096]{1,0:T(8,128)} async-done(((f32[96,512]{1,0:T(8,128)}), f32[96,4096]{1,0:T(8,128)}) %all-gather.10.cloned.1.call-update) | async-done | bytes 1572880 | tf_op jit(solution)/shard_map/all_gather | solution.py:38
  (224 shorter events, 181.4 us)
Async XLA Ops:
  7.2 18.6 %copy-start.43 = (s32[96]{0:T(128)S(1)}, s32[96]{0:T(128)}, u32[]{:S(2)}) copy-start(s32[96]{0:T(128)} %param.22) | copy-start | bytes 1156
  7.2 23.8 %copy-start.2 = (f32[1,6,3,96,512]{4,3,2,1,0:T(8,128)S(1)}, f32[1,6,3,96,512]{4,3,2,1,0:T(8,128)}, u32[]{:S(2)}) copy-start(f32[1,6,3,96,512]{4,3,2,1,0:T(8,128)} %param.33) | copy-start | bytes 10616836
  7.2 34.3 %all-gather.12.cloned.1.call-start = ((), (), s32[]{:S(2)}) async-start(), calls=%async_computation.5 | async-start | bytes 2359296 | tf_op jit(solution)/shard_map/all_gather | solution.py:38
  9.2 233.0 %all-gather.6.cloned.1.call-start = ((), (), s32[]{:S(2)}) async-start(), calls=%async_computation.2 | async-start | bytes 1769472 | tf_op jit(solution)/shard_map/all_gather | solution.py:38
  93.9 3.6 collective-permute-start
  99.1 36.6 %collective-permute-start.1 = (f32[96,4096]{1,0:T(8,128)S(1)}, f32[96,4096]{1,0:T(8,128)S(1)}, u32[]{:S(2)}, u32[]{:S(2)}) collective-permute-start(f32[96,4096]{1,0:T(8,128)S(1)} %add.257), channel_id=1, source_target_pairs={{0,2},{1,3},{2,0},{3,1},{4,6},{5,7},{6,4},{7,5},{8,10},{9,11},{10,... | collective-permute-start | bytes 4718600 | tf_op jit(solution)/shard_map/ppermute | solution.py:146
  135.9 70.3 %collective-permute-start.2 = (f32[96,4096]{1,0:T(8,128)S(1)}, f32[96,4096]{1,0:T(8,128)S(1)}, u32[]{:S(2)}, u32[]{:S(2)}) collective-permute-start(f32[96,4096]{1,0:T(8,128)S(1)} %add.258), channel_id=1, source_target_pairs={{0,4},{1,5},{2,6},{3,7},{4,0},{5,1},{6,2},{7,3},{8,12},{9,13},{10,... | collective-permute-start | bytes 4718600 | tf_op jit(solution)/shard_map/ppermute | solution.py:146
  265.8 34.1 %all-to-all-start = ((f32[32,17,288]{2,1,0:T(8,128)}), f32[32,17,288]{2,1,0:T(8,128)}, u32[]{:S(2)}, u32[]{:S(2)}) async-start(f32[32,17,288]{2,1,0:T(8,128)} %all_to_all.16), calls=%async_computation | async-start | bytes 2359296 | tf_op jit(solution)/shard_map/all_to_all | solution.py:121
  269.6 211.9 %all-gather.8.cloned.1.call-start = ((), (), s32[]{:S(2)}) async-start(), calls=%async_computation.3 | async-start | bytes 1769472 | tf_op jit(solution)/shard_map/all_gather | solution.py:38
  309.9 12.9 %copy-start.42 = (f32[96]{0:T(128)S(1)}, f32[96]{0:T(128)}, u32[]{:S(2)}) copy-start(f32[96]{0:T(128)} %multiply_select_fusion.1) | copy-start | bytes 1156
  335.0 3.6 collective-permute-start.3
  340.3 36.5 %collective-permute-start.4 = (f32[96,4096]{1,0:T(8,128)S(1)}, f32[96,4096]{1,0:T(8,128)S(1)}, u32[]{:S(2)}, u32[]{:S(2)}) collective-permute-start(f32[96,4096]{1,0:T(8,128)S(1)} %add.273), channel_id=1, source_target_pairs={{0,2},{1,3},{2,0},{3,1},{4,6},{5,7},{6,4},{7,5},{8,10},{9,11},{10,... | collective-permute-start | bytes 4718600 | tf_op jit(solution)/shard_map/ppermute | solution.py:146
  376.9 81.5 %copy-start.14 = (f32[3,96,512]{2,1,0:T(8,128)S(1)}, f32[3,96,512]{2,1,0:T(8,128)}, u32[]{:S(2)}) copy-start(f32[3,96,512]{2,1,0:T(8,128)} %get-tuple-element.3) | copy-start | bytes 1769476
  376.9 70.3 %collective-permute-start.5 = (f32[96,4096]{1,0:T(8,128)S(1)}, f32[96,4096]{1,0:T(8,128)S(1)}, u32[]{:S(2)}, u32[]{:S(2)}) collective-permute-start(f32[96,4096]{1,0:T(8,128)S(1)} %add.274), channel_id=1, source_target_pairs={{0,4},{1,5},{2,6},{3,7},{4,0},{5,1},{6,2},{7,3},{8,12},{9,13},{10,... | collective-permute-start | bytes 4718600 | tf_op jit(solution)/shard_map/ppermute | solution.py:146
  458.4 25.0 %copy-start.29 = (s32[2048]{0:T(1024)S(1)}, s32[2048]{0:T(1024)}, u32[]{:S(2)}) copy-start(s32[2048]{0:T(1024)} %pad_clamp_fusion) | copy-start | bytes 24580
  492.7 18.6 %copy-start.1 = (f32[1,6,3,96,512]{4,3,2,1,0:T(8,128)S(1)}, f32[1,6,3,96,512]{4,3,2,1,0:T(8,128)}, u32[]{:S(2)}) copy-start(f32[1,6,3,96,512]{4,3,2,1,0:T(8,128)} %param.34) | copy-start | bytes 10616836
  495.2 34.1 %all-to-all-start.1 = ((f32[32,17,288]{2,1,0:T(8,128)}), f32[32,17,288]{2,1,0:T(8,128)}, u32[]{:S(2)}, u32[]{:S(2)}) async-start(f32[32,17,288]{2,1,0:T(8,128)} %all_to_all.19), calls=%async_computation.1 | async-start | bytes 2359296 | tf_op jit(solution)/shard_map/all_to_all | solution.py:121
  499.0 212.0 %all-gather.10.cloned.1.call-start = ((), (), s32[]{:S(2)}) async-start(), calls=%async_computation.4 | async-start | bytes 1769472 | tf_op jit(solution)/shard_map/all_gather | solution.py:38
  511.3 19.4 %copy-start.35 = (s32[1024]{0:T(1024)S(1)}, s32[1024]{0:T(1024)}, u32[]{:S(2)}) copy-start(s32[1024]{0:T(1024)} %pad_clamp_fusion.1) | copy-start | bytes 12292
  540.5 11.8 %copy-start.41 = (f32[96]{0:T(128)S(1)}, f32[96]{0:T(128)}, u32[]{:S(2)}) copy-start(f32[96]{0:T(128)} %multiply_select_fusion) | copy-start | bytes 1156
  564.5 3.6 collective-permute-start.6
  569.8 36.5 %collective-permute-start.7 = (f32[96,4096]{1,0:T(8,128)S(1)}, f32[96,4096]{1,0:T(8,128)S(1)}, u32[]{:S(2)}, u32[]{:S(2)}) collective-permute-start(f32[96,4096]{1,0:T(8,128)S(1)} %add.285), channel_id=1, source_target_pairs={{0,2},{1,3},{2,0},{3,1},{4,6},{5,7},{6,4},{7,5},{8,10},{9,11},{10,... | collective-permute-start | bytes 4718600 | tf_op jit(solution)/shard_map/ppermute | solution.py:146
  606.4 70.3 %collective-permute-start.8 = (f32[96,4096]{1,0:T(8,128)S(1)}, f32[96,4096]{1,0:T(8,128)S(1)}, u32[]{:S(2)}, u32[]{:S(2)}) collective-permute-start(f32[96,4096]{1,0:T(8,128)S(1)} %add.286), channel_id=1, source_target_pairs={{0,4},{1,5},{2,6},{3,7},{4,0},{5,1},{6,2},{7,3},{8,12},{9,13},{10,... | collective-permute-start | bytes 4718600 | tf_op jit(solution)/shard_map/ppermute | solution.py:146
  687.9 24.9 %copy-start.30 = (s32[2048]{0:T(1024)S(1)}, s32[2048]{0:T(1024)}, u32[]{:S(2)}) copy-start(s32[2048]{0:T(1024)} %pad_clamp_fusion) | copy-start | bytes 24580
  (36 other events, 135.6 us)
Sparse Core Ops, SparseCore 0:
  9.6 31.8 all-gather.11
  217.5 24.6 all-gather.5
  458.6 22.9 all-gather.7
  688.0 22.9 all-gather.9
